TPU v7x, 128 devices: a whole 4x4x4 slice. The times are simulated.
128 devices in a mesh: seq: 8 (over z, core), head: 16 (over x, y).
Axes of the slice: x: 4, y: 4, z: 4, core: 2. Of those that a mesh axis runs over, the one named last changes fastest.
Arguments:
- lengths: int32 [16], replicated, may hold values from 128 to 8192, as said below
- page_owner: int32 [1536], replicated, may hold values from 0 to 16, as said below
- page_index: int32 [1536], replicated, may hold values from 0 to 127, as said below
- page_dest: int32 [1536], replicated, may hold values from 0 to 1535, as said below
- src_cache: bfloat16 [1536, 8, 64, 256], P(('seq', 'head')), may hold values from -8 to 8
- queries: bfloat16 [2, 16, 4096], replicated, may hold values from -8 to 8
- new_kv: bfloat16 [2, 16, 8, 256], replicated, may hold values from -6 to 6
- hidden_in: bfloat16 [2, 16, 4096], P(None, None, ('seq', 'head')), may hold values from -60 to 60
- out_weight: bfloat16 [4096, 4096], P(None, ('seq', 'head')), may hold values from -1.5 to 1.5
- norm_gain: bfloat16 [4096], P(('seq', 'head')), may hold values from 0.099609375 to 1.8984375
- router: bfloat16 [4096, 8], P(('seq', 'head')), may hold values from -0.09375 to 0.09375
- routes: int32 [2, 16, 2], replicated, may hold values from 0 to 7, all different within a row
- w_gate: bfloat16 [8, 4096, 8192], P('seq', None, 'head'), may hold values from -0.09375 to 0.09375
- w_up: bfloat16 [8, 4096, 8192], P('seq', None, 'head'), may hold values from -0.09375 to 0.09375
- w_down: bfloat16 [8, 8192, 4096], P('seq', 'head'), may hold values from -0.0625 to 0.0625
Outputs:
- page_pool: bfloat16 [16, 768, 64, 256], P('head', 'seq')
- mixed: bfloat16 [2, 16, 4096], P(None, None, ('seq', 'head'))
Inputs may be any that keep to these rules, and one draw needn't show every extreme that they name: Each length is at least 128; one equals 8192; the requests' pages, lengths[r] / 64 rounded up for request r, fit into the 1536 pages. `page_owner`: request r owns exactly lengths[r] / 64 rounded up source pages; the other pages carry 16. `page_index`: the pages of request r carry 0 to their count minus 1, each once; pages without request carry 0. `page_dest`: A permutation. Slot g belongs to destination group ((g % 768) // 96) * 2 + g // 768. Of the 12 pages that one device holds (pages i * 12 to (i + 1) * 12 - 1), at most 1 go to one group, and every draw has a device that sends exactly 1 to some group.
All inputs are finite; a program needn't handle non-finite values.
Results may differ from a plain program's by a relative error of at most 0.009.
Values may be sent and summed in bfloat16 or wider, within the bound.
A program may use at most 128 MiB of HBM per device.

v0:
```python
import jax
import jax.numpy as jnp
from jax import lax
from jax.sharding import Mesh
from jax.sharding import PartitionSpec as P

D = 4096
HQ = 32
KVH = 8
HD = 128
TOPK = 2
PAGE = 64
REQS = 16
SEQ = ("seq_0", "seq_1")
HEAD = ("head_0", "head_1")
SEQ_HEAD = ("seq_0", "seq_1", "head_0", "head_1")
NEG_FILL = -1e30
EPSILON = 1e-05
HIGHEST = lax.Precision.HIGHEST


def joined_all(array, axes, combine):
    for axis in axes:
        pieces = jax.tree.map(lambda part: lax.all_gather(part, axis), array)
        array = jax.tree.map(lambda part: part[0], pieces)
        for k in range(1, lax.axis_size(axis)):
            array = combine(array, jax.tree.map(lambda part: part[k], pieces))
    return array


def over_axes(array, axes):
    for axis in axes:
        array = lax.psum(array, axis)
    return array


def in_blocks(array, dim, peers):
    lengths = array.shape
    blocks = array.reshape(*lengths[:dim], peers, lengths[dim] // peers, *lengths[dim + 1 :])
    return jnp.moveaxis(blocks, dim, 0)


def cut_rows(length, count):
    unit = 8 if length >= 8 * count else 1
    return [length // unit * k // count * unit for k in range(1, count)]


def own_block(blocks, axes, sequence):
    lengths = [lax.axis_size(a) for a in axes]
    blocks = blocks.reshape(*lengths, *blocks.shape[1:])
    blocks = blocks.transpose(*sequence, *range(len(axes), blocks.ndim))
    blocks = blocks.reshape(-1, *blocks.shape[len(axes) :])
    for k in sequence:
        blocks = lax.psum_scatter(blocks, axes[k], scatter_dimension=0, tiled=True)
    return blocks[0]


def sum_all_axes_2(array, axes, dim):
    blocks = in_blocks(array, dim, lax.axis_size(axes))
    widest = max(range(1, max(2, blocks.ndim - 1)), key=lambda d: blocks.shape[d])
    count, gathered = (len(axes), [])
    for initial, share in enumerate(
        jnp.split(blocks, cut_rows(blocks.shape[widest], count), axis=widest)
    ):
        if share.size:
            sequence = [(initial + k) % count for k in range(count)]
            gathered.append(own_block(share, axes, sequence))
    return jnp.concatenate(gathered, axis=widest - 1)


def gate_mix(logits, picked):
    expert_ids = jnp.arange(logits.shape[1], dtype=jnp.int32)[None, :]
    first_hit = picked[:, 0:1] == expert_ids
    second_hit = picked[:, 1:2] == expert_ids
    first_logit = jnp.sum(jnp.where(first_hit, logits, 0.0), axis=1)
    second_logit = jnp.sum(jnp.where(second_hit, logits, 0.0), axis=1)
    leading = 1.0 / (1.0 + jnp.exp(second_logit - first_logit))
    trailing = 1.0 / (1.0 + jnp.exp(first_logit - second_logit))
    return jnp.where(first_hit, leading[:, None], 0.0) + jnp.where(
        second_hit, trailing[:, None], 0.0
    )


def combine(earlier, later):
    first_top, first_sum, first_acc = earlier
    second_top, second_sum, second_acc = later
    joint_top = jnp.maximum(first_top, second_top)
    first_factor = jnp.exp(first_top - joint_top)
    second_factor = jnp.exp(second_top - joint_top)
    return (
        joint_top,
        first_sum * first_factor + second_sum * second_factor,
        first_acc * first_factor[..., None] + second_acc * second_factor[..., None],
    )


def slot_plan(page_dest, pages_dev, slot_count, slots_dev, replicas, groups):
    part_index = page_dest // slot_count
    within = page_dest % slot_count
    target = within // slots_dev * replicas + part_index
    position = within % slots_dev
    per_device = target.reshape(-1, pages_dev)
    onehot = (per_device[:, :, None] == jnp.arange(groups, dtype=jnp.int32)[None, None, :]).astype(
        jnp.int32
    )
    before = jnp.cumsum(onehot, axis=1) - onehot
    ranking = jnp.sum(before * onehot, axis=2).reshape(-1)
    return (target, position, ranking)


def partial_attention(page_block, owners, page_pos, lengths, grouped, score_scale):
    head_dim = grouped.shape[-1]
    page_len = page_block.shape[2]
    requests = grouped.shape[1]
    clipped = jnp.minimum(owners, requests - 1)
    length_cap = jnp.take(lengths, clipped)
    offsets = page_pos[:, None] * page_len + jnp.arange(page_len, dtype=jnp.int32)[None, :]
    is_live = (owners < requests)[:, None] & (offsets < length_cap[:, None])
    live_mask = is_live[None, :, None, None, :]
    asked_rows = jnp.take(grouped, clipped, axis=1)
    scores = (
        jnp.einsum(
            "spkgd,pktd->spkgt",
            asked_rows,
            page_block[..., :head_dim],
            preferred_element_type=jnp.float32,
        )
        * score_scale
    )
    scores = jnp.where(live_mask, scores, NEG_FILL)
    members = owners[:, None] == jnp.arange(requests, dtype=jnp.int32)[None, :]
    page_top = jnp.max(scores, axis=4)
    row_top = jnp.max(
        jnp.where(members[None, :, :, None, None], page_top[:, :, None], NEG_FILL), axis=1
    )
    weights = jnp.where(
        live_mask, jnp.exp(scores - jnp.take(row_top, clipped, axis=1)[..., None]), 0.0
    )
    member_mask = members.astype(jnp.float32)
    totals = jnp.einsum("pr,spkg->srkg", member_mask, jnp.sum(weights, axis=4), precision=HIGHEST)
    page_out = jnp.einsum(
        "spkgt,pktd->spkgd",
        weights.astype(jnp.bfloat16),
        page_block[..., head_dim:],
        preferred_element_type=jnp.float32,
    )
    weighted = jnp.einsum("pr,spkgd->srkgd", member_mask, page_out, precision=HIGHEST)
    return (row_top, totals, weighted)


def body(
    lengths,
    page_owner,
    page_index,
    page_dest,
    src_cache,
    queries,
    new_kv,
    hidden_in,
    out_weight,
    norm_gain,
    router,
    routes,
    w_gate,
    w_up,
    w_down,
):
    seq_count = lax.axis_size(SEQ)
    head_count = lax.axis_size(HEAD)
    device_count = seq_count * head_count
    seq_pos = lax.axis_index(SEQ)
    head_pos = lax.axis_index(HEAD)
    pages_dev = src_cache.shape[0]
    page_total = page_dest.shape[0]
    replicas = head_count // KVH
    groups = seq_count * replicas
    slot_count = page_total // replicas
    slots_dev = pages_dev * KVH
    capacity = (slots_dev + device_count - 1) // device_count
    group_size = HQ // KVH
    step_count = queries.shape[0]
    row_count = step_count * REQS
    source = seq_pos * head_count + head_pos
    target, position, ranking = slot_plan(
        page_dest, pages_dev, slot_count, slots_dev, replicas, groups
    )
    local_target = lax.dynamic_slice_in_dim(target, source * pages_dev, pages_dev)
    local_rank = lax.dynamic_slice_in_dim(ranking, source * pages_dev, pages_dev)
    wanted = jnp.arange(groups * capacity, dtype=jnp.int32)
    matches = (local_target[None, :] == (wanted // capacity)[:, None]) & (
        local_rank[None, :] == (wanted % capacity)[:, None]
    )
    picked_page = jnp.sum(
        jnp.where(matches, jnp.arange(pages_dev, dtype=jnp.int32)[None, :], 0), axis=1
    )
    filled = jnp.any(matches, axis=1)
    packed = jnp.where(
        filled[:, None, None, None],
        jnp.take(src_cache, picked_page, axis=0),
        jnp.zeros((), jnp.bfloat16),
    )
    packed = packed.reshape(seq_count, replicas, capacity, KVH, PAGE, 2 * HD).transpose(
        0, 3, 1, 2, 4, 5
    )
    arrived = lax.all_to_all(
        packed.reshape(device_count, capacity, PAGE, 2 * HD),
        SEQ_HEAD,
        split_axis=0,
        concat_axis=0,
        tiled=True,
    )
    arrived = arrived.reshape(device_count * capacity, PAGE, 2 * HD)
    my_group = seq_pos * replicas + head_pos % replicas
    slot_ids = jnp.arange(slots_dev, dtype=jnp.int32)
    holders = (target[None, :] == my_group) & (position[None, :] == slot_ids[:, None])
    flat_index = jnp.arange(page_total, dtype=jnp.int32) // pages_dev * capacity + ranking
    chosen = jnp.sum(jnp.where(holders, flat_index[None, :], 0), axis=1)
    page_pool = jnp.take(arrived, chosen, axis=0)
    grouped = queries.reshape(step_count, REQS, KVH, group_size, HD)
    score_scale = HD ** (-0.5)
    kv_head = head_pos // replicas
    owners = jnp.sum(jnp.where(holders, page_owner[None, :], 0), axis=1)
    places = jnp.sum(jnp.where(holders, page_index[None, :], 0), axis=1)
    own_queries = lax.dynamic_slice_in_dim(grouped, kv_head, 1, axis=2)
    row_top, totals, weighted = partial_attention(
        page_pool[:, None], owners, places, lengths, own_queries, score_scale
    )
    owned_head = (jnp.arange(KVH, dtype=jnp.int32) == kv_head)[None, None, :, None]
    row_top = jnp.where(owned_head, row_top, NEG_FILL)
    totals = jnp.where(owned_head, totals, 0.0)
    weighted = jnp.where(owned_head[..., None], weighted, 0.0)
    row_top, totals, weighted = joined_all(
        (
            row_top.reshape(step_count, REQS, HQ),
            totals.reshape(step_count, REQS, HQ),
            weighted.reshape(step_count, REQS, HQ, HD),
        ),
        SEQ_HEAD,
        combine,
    )
    fresh_scores = (
        jnp.einsum(
            "srkgd,urkd->srkgu", grouped, new_kv[..., :HD], preferred_element_type=jnp.float32
        )
        * score_scale
    )
    causal = (jnp.arange(step_count)[:, None] >= jnp.arange(step_count)[None, :])[:, None, None, :]
    fresh_scores = jnp.where(
        causal, fresh_scores.reshape(step_count, REQS, HQ, step_count), NEG_FILL
    )
    joint_top = jnp.maximum(row_top, jnp.max(fresh_scores, axis=3))
    factor = jnp.exp(row_top - joint_top)
    fresh_weights = jnp.where(causal, jnp.exp(fresh_scores - joint_top[..., None]), 0.0)
    totals = totals * factor + jnp.sum(fresh_weights, axis=3)
    fresh_rounded = fresh_weights.reshape(step_count, REQS, KVH, group_size, step_count).astype(
        jnp.bfloat16
    )
    fresh_out = jnp.einsum(
        "srkgu,urkd->srkgd", fresh_rounded, new_kv[..., HD:], preferred_element_type=jnp.float32
    )
    weighted = weighted * factor[..., None] + fresh_out.reshape(step_count, REQS, HQ, HD)
    attended = (weighted / totals[..., None]).reshape(row_count, HQ * HD).astype(jnp.bfloat16)
    attn_out = jnp.dot(attended, out_weight, preferred_element_type=jnp.float32)
    middle = hidden_in.reshape(row_count, -1).astype(jnp.float32) + attn_out
    gain_row = norm_gain.astype(jnp.float32)[None, :]
    squares, routed = (
        over_axes(jnp.sum(middle * middle, axis=1), SEQ_HEAD),
        over_axes(
            jnp.dot(middle * gain_row, router.astype(jnp.float32), precision=HIGHEST), SEQ_HEAD
        ),
    )
    inverse_rms = lax.rsqrt(squares / D + EPSILON)
    logits = routed * inverse_rms[:, None]
    normed = (middle * inverse_rms[:, None] * gain_row).astype(jnp.bfloat16)
    features = lax.all_gather(normed, SEQ_HEAD, axis=1, tiled=True)
    mixture = gate_mix(logits, routes.reshape(row_count, TOPK))
    local_experts = w_gate.shape[0]
    local_mix = lax.dynamic_slice_in_dim(mixture, seq_pos * local_experts, local_experts, axis=1)
    gate_act = jnp.einsum("rd,edf->erf", features, w_gate, preferred_element_type=jnp.float32)
    upward = jnp.einsum("rd,edf->erf", features, w_up, preferred_element_type=jnp.float32)
    inner_act = (jax.nn.silu(gate_act) * upward).astype(jnp.bfloat16)
    produced = jnp.einsum("erf,efd->erd", inner_act, w_down, preferred_element_type=jnp.float32)
    moe_out = sum_all_axes_2(jnp.sum(local_mix.T[:, :, None] * produced, axis=0).T, SEQ_HEAD, 0)
    mixed = (middle + moe_out.T).astype(jnp.bfloat16).reshape(step_count, REQS, -1)
    return (page_pool[None], mixed)


def solution(mesh):
    split = Mesh(mesh.devices.reshape(4, 2, 4, 4), ("seq_0", "seq_1", "head_0", "head_1"))
    in_specs = (
        P(),
        P(),
        P(),
        P(),
        P(SEQ_HEAD, None, None, None),
        P(),
        P(),
        P(None, None, SEQ_HEAD),
        P(None, SEQ_HEAD),
        P(SEQ_HEAD),
        P(SEQ_HEAD, None),
        P(),
        P(SEQ, None, HEAD),
        P(SEQ, None, HEAD),
        P(SEQ, HEAD, None),
    )
    out_specs = (P(HEAD, SEQ, None, None), P(None, None, SEQ_HEAD))
    return jax.shard_map(body, mesh=split, in_specs=in_specs, out_specs=out_specs, check_vma=False)
```

profile of v0, /device:TPU:0, one launch (start us, length us, event | category | flops | bytes accessed | tf_op | source)
XLA Modules:
  0.0 609.9 jit_solution(12945465828086669318)
XLA Ops:
  16.9 11.7 %all-to-all-start = ((bf16[128,1,64,256]{3,2,1,0:T(8,128)(2,1)}), bf16[128,1,64,256]{3,2,1,0:T(8,128)(2,1)}, u32[]{:S(2)}, u32[]{:S(2)}) async-start(bf16[128,1,64,256]{3,2,1,0:T(8,128)(2,1)} %bitcast.483), calls=%async_computation | async-start | bytes 8388608 | tf_op jit(solution)/shard_map/all_to_all | solution.py:205
  41.7 38.0 %all-to-all-done = bf16[128,1,64,256]{3,2,1,0:T(8,128)(2,1)} async-done(((bf16[128,1,64,256]{3,2,1,0:T(8,128)(2,1)}), bf16[128,1,64,256]{3,2,1,0:T(8,128)(2,1)}, u32[]{:S(2)}, u32[]{:S(2)}) %all-to-all-start) | async-done | bytes 4194336 | tf_op jit(solution)/shard_map/all_to_all | solution.py:205
  92.8 12.2 %all_gather.49 = f32[4,2,16,32]{3,2,1,0:T(8,128)S(1)} all-gather(f32[1,2,16,32]{3,2,1,0:T(8,128)S(1)} %copy.236), channel_id=1, replica_groups=mesh['seq_0'=4,'seq_1'=2,'head_0'=4,'head_1'=4] {'seq_0'}, dimensions={0}, use_global_device_ids=true | all-gather | bytes 20480 | tf_op jit(solution)/shard_map/all_gather | solution.py:24
  105.0 14.8 %all-gather.5.cloned.1.call-done = f32[4,2,16,32,128]{4,3,2,1,0:T(8,128)} async-done(((f32[1,2,16,32,128]{4,3,2,1,0:T(8,128)}), f32[4,2,16,32,128]{4,3,2,1,0:T(8,128)}) %all-gather.5.cloned.1.call-update) | async-done | bytes 2097168 | tf_op jit(solution)/shard_map/all_gather | solution.py:24
  122.8 12.0 %all_gather.56 = f32[4,2,16,32]{3,2,1,0:T(8,128)S(1)} all-gather(f32[1,2,16,32]{3,2,1,0:T(8,128)S(1)} %copy.255), channel_id=1, replica_groups=mesh['seq_0'=4,'seq_1'=2,'head_0'=4,'head_1'=4] {'seq_0'}, dimensions={0}, use_global_device_ids=true | all-gather | bytes 20480 | tf_op jit(solution)/shard_map/all_gather | solution.py:24
  141.0 12.1 %all_gather.53 = f32[4,2,16,32]{3,2,1,0:T(8,128)S(1)} all-gather(f32[1,2,16,32]{3,2,1,0:T(8,128)S(1)} %get-tuple-element.32), channel_id=1, replica_groups=mesh['seq_0'=4,'seq_1'=2,'head_0'=4,'head_1'=4] {'head_0'}, dimensions={0}, use_global_device_ids=true | all-gather | bytes 20480 | tf_op jit(solution)/shard_map/all_gather | solution.py:24
  153.1 16.3 %all-gather.9.cloned.1.call-done = f32[4,2,16,32,128]{4,3,2,1,0:T(8,128)} async-done(((f32[1,2,16,32,128]{4,3,2,1,0:T(8,128)}), f32[4,2,16,32,128]{4,3,2,1,0:T(8,128)}) %all-gather.9.cloned.1.call-update) | async-done | bytes 2097168 | tf_op jit(solution)/shard_map/all_gather | solution.py:24
  175.3 11.9 %all_gather.58 = f32[4,2,16,32]{3,2,1,0:T(8,128)S(1)} all-gather(f32[1,2,16,32]{3,2,1,0:T(8,128)S(1)} %get-tuple-element.31), channel_id=1, replica_groups=mesh['seq_0'=4,'seq_1'=2,'head_0'=4,'head_1'=4] {'head_0'}, dimensions={0}, use_global_device_ids=true | all-gather | bytes 20480 | tf_op jit(solution)/shard_map/all_gather | solution.py:24
  187.1 13.0 %all_gather.55 = f32[4,2,16,32]{3,2,1,0:T(8,128)S(1)} all-gather(f32[1,2,16,32]{3,2,1,0:T(8,128)S(1)} %get-tuple-element.30), channel_id=1, replica_groups=mesh['seq_0'=4,'seq_1'=2,'head_0'=4,'head_1'=4] {'head_1'}, dimensions={0}, use_global_device_ids=true | all-gather | bytes 20480 | tf_op jit(solution)/shard_map/all_gather | solution.py:24
  201.5 11.9 %all_gather.59 = f32[4,2,16,32]{3,2,1,0:T(8,128)S(1)} all-gather(f32[1,2,16,32]{3,2,1,0:T(8,128)S(1)} %get-tuple-element.29), channel_id=1, replica_groups=mesh['seq_0'=4,'seq_1'=2,'head_0'=4,'head_1'=4] {'head_1'}, dimensions={0}, use_global_device_ids=true | all-gather | bytes 20480 | tf_op jit(solution)/shard_map/all_gather | solution.py:24
  222.3 10.7 %all-reduce.6 = (f32[32]{0:T(128)S(1)}, f32[32,8]{0,1:T(8,128)S(1)}) all-reduce(f32[32]{0:T(128)S(1)} %get-tuple-element.95, f32[32,8]{0,1:T(8,128)S(1)} %fusion.112), channel_id=1, replica_groups=mesh['seq_0'=4,'seq_1'=2,'head_0'=4,'head_1'=4] {'seq_0'}, use_global_device_ids=true, to_apply=%region_17.18 | all-reduce | flops 288 | bytes 2304 | tf_op jit(solution)/shard_map/psum | solution.py:33
  244.3 10.3 %all-reduce.4 = (f32[32]{0:T(128)S(1)}, f32[32,8]{0,1:T(8,128)S(1)}) all-reduce(f32[32]{0:T(128)S(1)} %get-tuple-element.11, f32[32,8]{0,1:T(8,128)S(1)} %get-tuple-element.12), channel_id=1, replica_groups=mesh['seq_0'=4,'seq_1'=2,'head_0'=4,'head_1'=4] {'head_1'}, use_global_device_ids=true, to_apply=%region_20.21 | all-reduce | flops 288 | bytes 2304 | tf_op jit(solution)/shard_map/psum | solution.py:33
  254.6 60.0 %all_gather.60 = bf16[32,4096]{0,1:T(8,128)(2,1)S(1)} all-gather(bf16[32,32]{0,1:T(8,128)(2,1)S(1)} %multiply_convert_fusion), channel_id=1, replica_groups=mesh['seq_0'=4,'seq_1'=2,'head_0'=4,'head_1'=4] {'seq_0','seq_1','head_0..., dimensions={1}, use_global_device_ids=true | all-gather | bytes 264192 | tf_op jit(solution)/shard_map/all_gather | solution.py:275
  335.4 15.0 %reduce-scatter.31.cloned.1.call-done = f32[32,8,32]{2,1,0:T(8,128)} async-done(((f32[128,8,32]{2,1,0:T(8,128)}), f32[32,8,32]{2,1,0:T(8,128)}) %reduce-scatter.31.cloned.1.call-update) | async-done | bytes 32784 | tf_op jit(solution)/shard_map/reduce_scatter | solution.py:54
  350.4 23.5 %reduce-scatter.25.cloned.1.call-done = f32[32,8,32]{2,1,0:T(8,128)} async-done(((f32[128,8,32]{2,1,0:T(8,128)}), f32[32,8,32]{2,1,0:T(8,128)}) %reduce-scatter.25.cloned.1.call-update) | async-done | bytes 32784 | tf_op jit(solution)/shard_map/reduce_scatter | solution.py:54
  374.0 32.0 %reduce-scatter.13.cloned.1.call-done = f32[32,8,32]{1,0,2:T(8,128)} async-done(((f32[128,8,32]{1,0,2:T(8,128)}), f32[32,8,32]{1,0,2:T(8,128)}) %reduce-scatter.13.cloned.1.call-update) | async-done | bytes 32784 | tf_op jit(solution)/shard_map/reduce_scatter | solution.py:54
  408.2 20.8 %reduce-scatter.33.cloned.1.call-done = f32[8,8,32]{2,1,0:T(8,128)} async-done(((f32[32,8,32]{2,1,0:T(8,128)}), f32[8,8,32]{2,1,0:T(8,128)}) %reduce-scatter.33.cloned.1.call-update) | async-done | bytes 8208 | tf_op jit(solution)/shard_map/reduce_scatter | solution.py:54
  429.0 22.5 %reduce-scatter.27.cloned.1.call-done = f32[8,8,32]{2,1,0:T(8,128)} async-done(((f32[32,8,32]{2,1,0:T(8,128)}), f32[8,8,32]{2,1,0:T(8,128)}) %reduce-scatter.27.cloned.1.call-update) | async-done | bytes 8208 | tf_op jit(solution)/shard_map/reduce_scatter | solution.py:54
  478.3 13.6 %reduce-scatter.35.cloned.1.call-done = f32[4,8,32]{2,1,0:T(8,128)} async-done(((f32[8,8,32]{2,1,0:T(8,128)}), f32[4,8,32]{2,1,0:T(8,128)}) %reduce-scatter.35.cloned.1.call-update) | async-done | bytes 4112 | tf_op jit(solution)/shard_map/reduce_scatter | solution.py:54
  491.9 17.7 %all-reduce.3 = f32[4,8,32]{2,1,0:T(8,128)S(1)} all-reduce(f32[4,8,32]{2,1,0:T(8,128)} %reduce-scatter.35.cloned.1.call-done), channel_id=17, replica_groups=mesh['seq_0'=4,'seq_1'=2,'head_0'=4,'head_1'=4] {'head_0'}, use_global_device_ids=true, to_apply=%region_38.39.clone | all-reduce | flops 1024 | bytes 8192
  519.8 19.1 %reduce-scatter.17.cloned.1.call-done = f32[4,8,32]{2,1,0:T(8,128)} async-done(((f32[16,8,32]{2,1,0:T(8,128)}), f32[4,8,32]{2,1,0:T(8,128)}) %reduce-scatter.17.cloned.1.call-update) | async-done | bytes 4112 | tf_op jit(solution)/shard_map/reduce_scatter | solution.py:54
  538.8 17.5 %all-reduce = f32[4,8,32]{2,1,0:T(8,128)S(1)} all-reduce(f32[4,8,32]{2,1,0:T(8,128)} %reduce-scatter.17.cloned.1.call-done), channel_id=5, replica_groups=mesh['seq_0'=4,'seq_1'=2,'head_0'=4,'head_1'=4] {'head_1'}, use_global_device_ids=true, to_apply=%region_26.27.clone | all-reduce | flops 1024 | bytes 8192
  562.3 22.0 %reduce-scatter.23.cloned.1.call-done = f32[4,8,32]{2,1,0:T(8,128)} async-done(((f32[16,8,32]{2,1,0:T(8,128)}), f32[4,8,32]{2,1,0:T(8,128)}) %reduce-scatter.23.cloned.1.call-update) | async-done | bytes 4112 | tf_op jit(solution)/shard_map/reduce_scatter | solution.py:54
  584.3 17.7 %all-reduce.1 = f32[4,8,32]{2,1,0:T(8,128)S(1)} all-reduce(f32[4,8,32]{2,1,0:T(8,128)} %reduce-scatter.23.cloned.1.call-done), channel_id=9, replica_groups=mesh['seq_0'=4,'seq_1'=2,'head_0'=4,'head_1'=4] {'seq_0'}, use_global_device_ids=true, to_apply=%region_30.31.clone | all-reduce | flops 1024 | bytes 8192
  (225 shorter events, 139.1 us)
Async XLA Ops:
  16.9 62.8 %all-to-all-start = ((bf16[128,1,64,256]{3,2,1,0:T(8,128)(2,1)}), bf16[128,1,64,256]{3,2,1,0:T(8,128)(2,1)}, u32[]{:S(2)}, u32[]{:S(2)}) async-start(bf16[128,1,64,256]{3,2,1,0:T(8,128)(2,1)} %bitcast.483), calls=%async_computation | async-start | bytes 8388608 | tf_op jit(solution)/shard_map/all_to_all | solution.py:205
  28.6 91.2 %all-gather.5.cloned.1.call-start = ((), (), s32[]{:S(2)}) async-start(), calls=%async_computation.13 | async-start | bytes 2621440 | tf_op jit(solution)/shard_map/all_gather | solution.py:24
  91.7 45.0 %all-gather.7.cloned.1.call-start = ((), (), s32[]{:S(2)}) async-start(), calls=%async_computation.14 | async-start | bytes 1572864 | tf_op jit(solution)/shard_map/all_gather | solution.py:24
  122.7 49.7 %copy-start.11 = (bf16[2,16,32]{2,1,0:T(8,128)(2,1)S(1)}, bf16[2,16,32]{2,1,0:T(8,128)(2,1)}, u32[]{:S(2)}) copy-start(bf16[2,16,32]{2,1,0:T(8,128)(2,1)} %param.22) | copy-start | bytes 6148
  122.7 46.8 %all-gather.9.cloned.1.call-start = ((), (), s32[]{:S(2)}) async-start(), calls=%async_computation.15 | async-start | bytes 2621440 | tf_op jit(solution)/shard_map/all_gather | solution.py:24
  139.1 76.0 %all-gather.11.cloned.1.call-start = ((), (), s32[]{:S(2)}) async-start(), calls=%async_computation.16 | async-start | bytes 2621440 | tf_op jit(solution)/shard_map/all_gather | solution.py:24
  172.3 178.0 %reduce-scatter.31.cloned.1.call-start = ((), (), s32[]{:S(2)}) async-start(), calls=%async_computation.26 | async-start | bytes 655360 | tf_op jit(solution)/shard_map/reduce_scatter | solution.py:54
  331.4 74.7 %copy-start.3 = (f32[128,8,32]{1,0,2:T(8,128)S(1)}, f32[128,8,32]{1,0,2:T(8,128)}, u32[]{:S(2)}) copy-start(f32[128,8,32]{1,0,2:T(8,128)} %get-tuple-element.40) | copy-start | bytes 393220
  331.4 42.6 %reduce-scatter.25.cloned.1.call-start = ((), (), s32[]{:S(2)}) async-start(), calls=%async_computation.23 | async-start | bytes 655360 | tf_op jit(solution)/shard_map/reduce_scatter | solution.py:54
  334.5 117.1 %copy-start.20 = (u32[128]{0:T(128)S(1)}, u32[128]{0:T(128)}, u32[]{:S(2)}) copy-start(u32[128]{0:T(128)} %constant.244) | copy-start | bytes 1540
  334.6 117.7 %copy-start.19 = (u32[128]{0:T(128)S(1)}, u32[128]{0:T(128)}, u32[]{:S(2)}) copy-start(u32[128]{0:T(128)} %constant.240) | copy-start | bytes 1540
  334.6 118.3 %copy-start.18 = (u32[128]{0:T(128)S(1)}, u32[128]{0:T(128)}, u32[]{:S(2)}) copy-start(u32[128]{0:T(128)} %constant.236) | copy-start | bytes 1540
  334.6 118.9 %copy-start.17 = (u32[128]{0:T(128)S(1)}, u32[128]{0:T(128)}, u32[]{:S(2)}) copy-start(u32[128]{0:T(128)} %constant.232) | copy-start | bytes 1540
  334.6 71.5 %reduce-scatter.13.cloned.1.call-start = ((), (), s32[]{:S(2)}) async-start(), calls=%async_computation.17 | async-start | bytes 2621440 | tf_op jit(solution)/shard_map/reduce_scatter | solution.py:54
  335.3 93.6 %reduce-scatter.33.cloned.1.call-start = ((), (), s32[]{:S(2)}) async-start(), calls=%async_computation.27 | async-start | bytes 163840 | tf_op jit(solution)/shard_map/reduce_scatter | solution.py:54
  350.4 101.2 %reduce-scatter.27.cloned.1.call-start = ((), (), s32[]{:S(2)}) async-start(), calls=%async_computation.24 | async-start | bytes 163840 | tf_op jit(solution)/shard_map/reduce_scatter | solution.py:54
  374.0 89.9 %reduce-scatter.15.cloned.1.call-start = ((), (), s32[]{:S(2)}) async-start(), calls=%async_computation.18 | async-start | bytes 786432 | tf_op jit(solution)/shard_map/reduce_scatter | solution.py:54
  406.1 72.1 %reduce-scatter.19.cloned.1.call-start = ((), (), s32[]{:S(2)}) async-start(), calls=%async_computation.20 | async-start | bytes 786432 | tf_op jit(solution)/shard_map/reduce_scatter | solution.py:54
  408.1 83.8 %reduce-scatter.35.cloned.1.call-start = ((), (), s32[]{:S(2)}) async-start(), calls=%async_computation.28 | async-start | bytes 49152 | tf_op jit(solution)/shard_map/reduce_scatter | solution.py:54
  429.0 87.6 %reduce-scatter.29.cloned.1.call-start = ((), (), s32[]{:S(2)}) async-start(), calls=%async_computation.25 | async-start | bytes 40960 | tf_op jit(solution)/shard_map/reduce_scatter | solution.py:54
  451.6 87.3 %reduce-scatter.17.cloned.1.call-start = ((), (), s32[]{:S(2)}) async-start(), calls=%async_computation.19 | async-start | bytes 81920 | tf_op jit(solution)/shard_map/reduce_scatter | solution.py:54
  465.7 137.7 %copy-start.1 = (bf16[12,8,64,256]{3,2,1,0:T(8,128)(2,1)S(1)}, bf16[12,8,64,256]{3,2,1,0:T(8,128)(2,1)}, u32[]{:S(2)}) copy-start(bf16[12,8,64,256]{3,2,1,0:T(8,128)(2,1)} %param.19) | copy-start | bytes 9437188
  465.7 96.0 %reduce-scatter.21.cloned.1.call-start = ((), (), s32[]{:S(2)}) async-start(), calls=%async_computation.21 | async-start | bytes 327680 | tf_op jit(solution)/shard_map/reduce_scatter | solution.py:54
  478.2 106.0 %reduce-scatter.23.cloned.1.call-start = ((), (), s32[]{:S(2)}) async-start(), calls=%async_computation.22 | async-start | bytes 81920 | tf_op jit(solution)/shard_map/reduce_scatter | solution.py:54
  (14 other events, 198.3 us)
Sparse Core Ops, SparseCore 0:
  91.8 27.9 all-gather.4
  122.8 11.3 all-gather.6
  139.2 30.1 all-gather.8
  172.5 31.3 all-gather.10
  331.5 18.7 reduce-scatter.30
  352.6 21.3 reduce-scatter.24
  376.4 29.6 reduce-scatter.12
  408.4 20.4 reduce-scatter.32
  431.3 20.1 reduce-scatter.26
  453.7 10.1 reduce-scatter.14
  466.3 11.8 reduce-scatter.18
  480.4 11.5 reduce-scatter.34
  494.3 22.2 reduce-scatter.28
  518.7 20.0 reduce-scatter.16
  541.1 20.5 reduce-scatter.20
  563.9 20.3 reduce-scatter.22
where the time goes:
time: 611 us; the launch traced here: 610 us
  waiting for transfers between devices  268 us (44%)
  blocking collectives  224 us (37%)
  local copies, waits for them, and re-layouts  42 us (7%)
  other arithmetic  29.7 us (5%)
  matrix products  18.5 us (3%)
  between operations  14.7 us (2%)
  starting transfers between devices  12.4 us (2%)
    reduce_scatter x12, waiting for transfers between devices, own_block(): blocks = lax.psum_scatter(blocks, axes[k], scatter_dimension=0, tiled=True)  198 us
    all_gather x8, blocking collectives, joined_all(): pieces = jax.tree.map(lambda part: lax.all_gather(part, axis), array)  76.6 us
    all_gather x1, blocking collectives, body(): features = lax.all_gather(normed, SEQ_HEAD, axis=1, tiled=True)  60 us
    unnamed x4, blocking collectives  55.5 us
    all_to_all x1, waiting for transfers between devices, body(): lax.all_to_all(packed.reshape(device_count, capacity, PAGE, 2 * HD), SEQ_...  38 us
    psum x4, blocking collectives, over_axes(): array = lax.psum(array, axis)  32.2 us
    all_gather x4, waiting for transfers between devices, joined_all(): pieces = jax.tree.map(lambda part: lax.all_gather(part, axis), array)  31.1 us
  transfers between devices with their start and end apart: 17, of which 15 were waited for; matrix products, arithmetic and copies ran while one was open for 6% of the time, Pallas kernels for 0%

commit v1 on v0

--- a/solution.py
+++ b/solution.py
@@ -3,6 +3,7 @@
 from jax import lax
 from jax.sharding import Mesh
 from jax.sharding import PartitionSpec as P
+from jax.lax import all_to_all, psum
 
 D = 4096
 HQ = 32
@@ -272,7 +273,15 @@
     inverse_rms = lax.rsqrt(squares / D + EPSILON)
     logits = routed * inverse_rms[:, None]
     normed = (middle * inverse_rms[:, None] * gain_row).astype(jnp.bfloat16)
-    features = lax.all_gather(normed, SEQ_HEAD, axis=1, tiled=True)
+    features = jnp.concatenate(
+        all_to_all(
+            jnp.stack([normed for _ in range(psum(1, axis_name=SEQ_HEAD))], axis=0),
+            concat_axis=0,
+            split_axis=0,
+            axis_name=SEQ_HEAD,
+        ),
+        axis=1,
+    )
     mixture = gate_mix(logits, routes.reshape(row_count, TOPK))
     local_experts = w_gate.shape[0]
     local_mix = lax.dynamic_slice_in_dim(mixture, seq_pos * local_experts, local_experts, axis=1)

time: 611 us -> 569 us (0.931)
  blocking collectives: 224 us -> 164 us
  waiting for transfers between devices: 268 us -> 278 us
    all_gather x1 -> x0, blocking collectives: 60 us -> none  [body(): features = lax.all_gather(normed, SEQ_HEAD, axis=1, tiled=True)]
    all_to_all x0 -> x1, waiting for transfers between devices: none -> 10.5 us  [body(): all_to_all(jnp.stack([normed for _ in range(psum(1, axis_name=SEQ_HEAD))]...]
  transfers between devices with their start and end apart: 17 -> 18, of which waited for: 15 -> 16; matrix products, arithmetic and copies ran while one was open for 6% -> 6% of each run, Pallas kernels for 0% -> 0%
where the time goes in v1:
time: 569 us; the launch traced here: 568 us
  waiting for transfers between devices  278 us (49%)
  blocking collectives  164 us (29%)
  local copies, waits for them, and re-layouts  45.7 us (8%)
  other arithmetic  29.7 us (5%)
  matrix products  18.5 us (3%)
  starting transfers between devices  17.2 us (3%)
  between operations  14.7 us (3%)
    reduce_scatter x12, waiting for transfers between devices, own_block(): blocks = lax.psum_scatter(blocks, axes[k], scatter_dimension=0, tiled=True)  197 us
    all_gather x8, blocking collectives, joined_all(): pieces = jax.tree.map(lambda part: lax.all_gather(part, axis), array)  76.6 us
    unnamed x4, blocking collectives  55.4 us
    all_to_all x1, waiting for transfers between devices, body(): lax.all_to_all(packed.reshape(device_count, capacity, PAGE, 2 * HD), SEQ_...  38 us
    psum x4, blocking collectives, over_axes(): array = lax.psum(array, axis)  32.2 us
    all_gather x4, waiting for transfers between devices, joined_all(): pieces = jax.tree.map(lambda part: lax.all_gather(part, axis), array)  31.1 us
    all_to_all x1, starting transfers between devices, body(): lax.all_to_all(packed.reshape(device_count, capacity, PAGE, 2 * HD), SEQ_...  11.7 us
  transfers between devices with their start and end apart: 18, of which 16 were waited for; matrix products, arithmetic and copies ran while one was open for 6% of the time, Pallas kernels for 0%

profile of v1, /device:TPU:0, one launch (start us, length us, event | category | flops | bytes accessed | tf_op | source)
XLA Modules:
  0.0 567.7 jit_solution(5347149212515532319)
XLA Ops:
  16.9 11.7 %all-to-all-start = ((bf16[128,1,64,256]{3,2,1,0:T(8,128)(2,1)}), bf16[128,1,64,256]{3,2,1,0:T(8,128)(2,1)}, u32[]{:S(2)}, u32[]{:S(2)}) async-start(bf16[128,1,64,256]{3,2,1,0:T(8,128)(2,1)} %bitcast.484), calls=%async_computation | async-start | bytes 8388608 | tf_op jit(solution)/shard_map/all_to_all | solution.py:206
  41.7 38.0 %all-to-all-done = bf16[128,1,64,256]{3,2,1,0:T(8,128)(2,1)} async-done(((bf16[128,1,64,256]{3,2,1,0:T(8,128)(2,1)}), bf16[128,1,64,256]{3,2,1,0:T(8,128)(2,1)}, u32[]{:S(2)}, u32[]{:S(2)}) %all-to-all-start) | async-done | bytes 4194336 | tf_op jit(solution)/shard_map/all_to_all | solution.py:206
  92.8 12.2 %all_gather.46 = f32[4,2,16,32]{3,2,1,0:T(8,128)S(1)} all-gather(f32[1,2,16,32]{3,2,1,0:T(8,128)S(1)} %copy.245), channel_id=1, replica_groups=mesh['seq_0'=4,'seq_1'=2,'head_0'=4,'head_1'=4] {'seq_0'}, dimensions={0}, use_global_device_ids=true | all-gather | bytes 20480 | tf_op jit(solution)/shard_map/all_gather | solution.py:25
  105.0 14.8 %all-gather.5.cloned.1.call-done = f32[4,2,16,32,128]{4,3,2,1,0:T(8,128)} async-done(((f32[1,2,16,32,128]{4,3,2,1,0:T(8,128)}), f32[4,2,16,32,128]{4,3,2,1,0:T(8,128)}) %all-gather.5.cloned.1.call-update) | async-done | bytes 2097168 | tf_op jit(solution)/shard_map/all_gather | solution.py:25
  122.8 12.0 %all_gather.53 = f32[4,2,16,32]{3,2,1,0:T(8,128)S(1)} all-gather(f32[1,2,16,32]{3,2,1,0:T(8,128)S(1)} %copy.264), channel_id=1, replica_groups=mesh['seq_0'=4,'seq_1'=2,'head_0'=4,'head_1'=4] {'seq_0'}, dimensions={0}, use_global_device_ids=true | all-gather | bytes 20480 | tf_op jit(solution)/shard_map/all_gather | solution.py:25
  141.0 12.1 %all_gather.50 = f32[4,2,16,32]{3,2,1,0:T(8,128)S(1)} all-gather(f32[1,2,16,32]{3,2,1,0:T(8,128)S(1)} %get-tuple-element.32), channel_id=1, replica_groups=mesh['seq_0'=4,'seq_1'=2,'head_0'=4,'head_1'=4] {'head_0'}, dimensions={0}, use_global_device_ids=true | all-gather | bytes 20480 | tf_op jit(solution)/shard_map/all_gather | solution.py:25
  153.1 16.3 %all-gather.9.cloned.1.call-done = f32[4,2,16,32,128]{4,3,2,1,0:T(8,128)} async-done(((f32[1,2,16,32,128]{4,3,2,1,0:T(8,128)}), f32[4,2,16,32,128]{4,3,2,1,0:T(8,128)}) %all-gather.9.cloned.1.call-update) | async-done | bytes 2097168 | tf_op jit(solution)/shard_map/all_gather | solution.py:25
  175.2 11.9 %all_gather.55 = f32[4,2,16,32]{3,2,1,0:T(8,128)S(1)} all-gather(f32[1,2,16,32]{3,2,1,0:T(8,128)S(1)} %get-tuple-element.31), channel_id=1, replica_groups=mesh['seq_0'=4,'seq_1'=2,'head_0'=4,'head_1'=4] {'head_0'}, dimensions={0}, use_global_device_ids=true | all-gather | bytes 20480 | tf_op jit(solution)/shard_map/all_gather | solution.py:25
  187.1 12.8 %all_gather.52 = f32[4,2,16,32]{3,2,1,0:T(8,128)S(1)} all-gather(f32[1,2,16,32]{3,2,1,0:T(8,128)S(1)} %get-tuple-element.30), channel_id=1, replica_groups=mesh['seq_0'=4,'seq_1'=2,'head_0'=4,'head_1'=4] {'head_1'}, dimensions={0}, use_global_device_ids=true | all-gather | bytes 20480 | tf_op jit(solution)/shard_map/all_gather | solution.py:25
  201.3 12.0 %all_gather.56 = f32[4,2,16,32]{3,2,1,0:T(8,128)S(1)} all-gather(f32[1,2,16,32]{3,2,1,0:T(8,128)S(1)} %get-tuple-element.29), channel_id=1, replica_groups=mesh['seq_0'=4,'seq_1'=2,'head_0'=4,'head_1'=4] {'head_1'}, dimensions={0}, use_global_device_ids=true | all-gather | bytes 20480 | tf_op jit(solution)/shard_map/all_gather | solution.py:25
  222.3 10.7 %all-reduce.6 = (f32[32]{0:T(128)S(1)}, f32[32,8]{0,1:T(8,128)S(1)}) all-reduce(f32[32]{0:T(128)S(1)} %get-tuple-element.95, f32[32,8]{0,1:T(8,128)S(1)} %fusion.112), channel_id=1, replica_groups=mesh['seq_0'=4,'seq_1'=2,'head_0'=4,'head_1'=4] {'seq_0'}, use_global_device_ids=true, to_apply=%region_17.18 | all-reduce | flops 288 | bytes 2304 | tf_op jit(solution)/shard_map/psum | solution.py:34
  244.2 10.3 %all-reduce.4 = (f32[32]{0:T(128)S(1)}, f32[32,8]{0,1:T(8,128)S(1)}) all-reduce(f32[32]{0:T(128)S(1)} %get-tuple-element.11, f32[32,8]{0,1:T(8,128)S(1)} %get-tuple-element.12), channel_id=1, replica_groups=mesh['seq_0'=4,'seq_1'=2,'head_0'=4,'head_1'=4] {'head_1'}, use_global_device_ids=true, to_apply=%region_20.21 | all-reduce | flops 288 | bytes 2304 | tf_op jit(solution)/shard_map/psum | solution.py:34
  261.3 10.5 %all-to-all-done.1 = bf16[128,2,512]{2,1,0:T(2,128)(2,1)S(1)} async-done(((bf16[128,2,512]{2,1,0:T(2,128)(2,1)}), bf16[128,2,512]{2,1,0:T(2,128)(2,1)S(1)}, u32[]{:S(2)}, u32[]{:S(2)}) %all-to-all-start.1) | async-done | bytes 262176 | tf_op jit(solution)/shard_map/all_to_all | solution.py:277
  294.5 13.7 %reduce-scatter.31.cloned.1.call-done = f32[32,8,32]{2,1,0:T(8,128)} async-done(((f32[128,8,32]{2,1,0:T(8,128)}), f32[32,8,32]{2,1,0:T(8,128)}) %reduce-scatter.31.cloned.1.call-update) | async-done | bytes 32784 | tf_op jit(solution)/shard_map/reduce_scatter | solution.py:55
  308.2 23.5 %reduce-scatter.25.cloned.1.call-done = f32[32,8,32]{2,1,0:T(8,128)} async-done(((f32[128,8,32]{2,1,0:T(8,128)}), f32[32,8,32]{2,1,0:T(8,128)}) %reduce-scatter.25.cloned.1.call-update) | async-done | bytes 32784 | tf_op jit(solution)/shard_map/reduce_scatter | solution.py:55
  331.8 32.0 %reduce-scatter.13.cloned.1.call-done = f32[32,8,32]{1,0,2:T(8,128)} async-done(((f32[128,8,32]{1,0,2:T(8,128)}), f32[32,8,32]{1,0,2:T(8,128)}) %reduce-scatter.13.cloned.1.call-update) | async-done | bytes 32784 | tf_op jit(solution)/shard_map/reduce_scatter | solution.py:55
  365.9 20.8 %reduce-scatter.33.cloned.1.call-done = f32[8,8,32]{2,1,0:T(8,128)} async-done(((f32[32,8,32]{2,1,0:T(8,128)}), f32[8,8,32]{2,1,0:T(8,128)}) %reduce-scatter.33.cloned.1.call-update) | async-done | bytes 8208 | tf_op jit(solution)/shard_map/reduce_scatter | solution.py:55
  386.8 22.5 %reduce-scatter.27.cloned.1.call-done = f32[8,8,32]{2,1,0:T(8,128)} async-done(((f32[32,8,32]{2,1,0:T(8,128)}), f32[8,8,32]{2,1,0:T(8,128)}) %reduce-scatter.27.cloned.1.call-update) | async-done | bytes 8208 | tf_op jit(solution)/shard_map/reduce_scatter | solution.py:55
  436.1 13.6 %reduce-scatter.35.cloned.1.call-done = f32[4,8,32]{2,1,0:T(8,128)} async-done(((f32[8,8,32]{2,1,0:T(8,128)}), f32[4,8,32]{2,1,0:T(8,128)}) %reduce-scatter.35.cloned.1.call-update) | async-done | bytes 4112 | tf_op jit(solution)/shard_map/reduce_scatter | solution.py:55
  449.7 17.6 %all-reduce.3 = f32[4,8,32]{2,1,0:T(8,128)S(1)} all-reduce(f32[4,8,32]{2,1,0:T(8,128)} %reduce-scatter.35.cloned.1.call-done), channel_id=17, replica_groups=mesh['seq_0'=4,'seq_1'=2,'head_0'=4,'head_1'=4] {'head_0'}, use_global_device_ids=true, to_apply=%region_38.39.clone | all-reduce | flops 1024 | bytes 8192
  477.6 19.1 %reduce-scatter.17.cloned.1.call-done = f32[4,8,32]{2,1,0:T(8,128)} async-done(((f32[16,8,32]{2,1,0:T(8,128)}), f32[4,8,32]{2,1,0:T(8,128)}) %reduce-scatter.17.cloned.1.call-update) | async-done | bytes 4112 | tf_op jit(solution)/shard_map/reduce_scatter | solution.py:55
  496.7 17.5 %all-reduce = f32[4,8,32]{2,1,0:T(8,128)S(1)} all-reduce(f32[4,8,32]{2,1,0:T(8,128)} %reduce-scatter.17.cloned.1.call-done), channel_id=5, replica_groups=mesh['seq_0'=4,'seq_1'=2,'head_0'=4,'head_1'=4] {'head_1'}, use_global_device_ids=true, to_apply=%region_26.27.clone | all-reduce | flops 1024 | bytes 8192
  520.1 22.0 %reduce-scatter.23.cloned.1.call-done = f32[4,8,32]{2,1,0:T(8,128)} async-done(((f32[16,8,32]{2,1,0:T(8,128)}), f32[4,8,32]{2,1,0:T(8,128)}) %reduce-scatter.23.cloned.1.call-update) | async-done | bytes 4112 | tf_op jit(solution)/shard_map/reduce_scatter | solution.py:55
  542.0 17.7 %all-reduce.1 = f32[4,8,32]{2,1,0:T(8,128)S(1)} all-reduce(f32[4,8,32]{2,1,0:T(8,128)} %reduce-scatter.23.cloned.1.call-done), channel_id=9, replica_groups=mesh['seq_0'=4,'seq_1'=2,'head_0'=4,'head_1'=4] {'seq_0'}, use_global_device_ids=true, to_apply=%region_30.31.clone | all-reduce | flops 1024 | bytes 8192
  (232 shorter events, 147.7 us)
Async XLA Ops:
  16.9 62.8 %all-to-all-start = ((bf16[128,1,64,256]{3,2,1,0:T(8,128)(2,1)}), bf16[128,1,64,256]{3,2,1,0:T(8,128)(2,1)}, u32[]{:S(2)}, u32[]{:S(2)}) async-start(bf16[128,1,64,256]{3,2,1,0:T(8,128)(2,1)} %bitcast.484), calls=%async_computation | async-start | bytes 8388608 | tf_op jit(solution)/shard_map/all_to_all | solution.py:206
  28.6 91.2 %all-gather.5.cloned.1.call-start = ((), (), s32[]{:S(2)}) async-start(), calls=%async_computation.14 | async-start | bytes 2621440 | tf_op jit(solution)/shard_map/all_gather | solution.py:25
  91.7 45.0 %all-gather.7.cloned.1.call-start = ((), (), s32[]{:S(2)}) async-start(), calls=%async_computation.15 | async-start | bytes 1572864 | tf_op jit(solution)/shard_map/all_gather | solution.py:25
  122.7 46.8 %all-gather.9.cloned.1.call-start = ((), (), s32[]{:S(2)}) async-start(), calls=%async_computation.16 | async-start | bytes 2621440 | tf_op jit(solution)/shard_map/all_gather | solution.py:25
  139.1 75.9 %all-gather.11.cloned.1.call-start = ((), (), s32[]{:S(2)}) async-start(), calls=%async_computation.17 | async-start | bytes 2621440 | tf_op jit(solution)/shard_map/all_gather | solution.py:25
  256.3 15.5 %all-to-all-start.1 = ((bf16[128,2,512]{2,1,0:T(2,128)(2,1)}), bf16[128,2,512]{2,1,0:T(2,128)(2,1)S(1)}, u32[]{:S(2)}, u32[]{:S(2)}) async-start(bf16[128,2,512]{2,1,0:T(2,128)(2,1)} %reshape.896), calls=%async_computation.1 | async-start | bytes 524288 | tf_op jit(solution)/shard_map/all_to_all | solution.py:277
  260.9 47.2 %reduce-scatter.31.cloned.1.call-start = ((), (), s32[]{:S(2)}) async-start(), calls=%async_computation.27 | async-start | bytes 655360 | tf_op jit(solution)/shard_map/reduce_scatter | solution.py:55
  290.5 73.4 %copy-start.3 = (f32[128,8,32]{1,0,2:T(8,128)S(1)}, f32[128,8,32]{1,0,2:T(8,128)}, u32[]{:S(2)}) copy-start(f32[128,8,32]{1,0,2:T(8,128)} %get-tuple-element.40) | copy-start | bytes 393220
  290.5 41.2 %reduce-scatter.25.cloned.1.call-start = ((), (), s32[]{:S(2)}) async-start(), calls=%async_computation.24 | async-start | bytes 655360 | tf_op jit(solution)/shard_map/reduce_scatter | solution.py:55
  293.6 115.8 %copy-start.20 = (u32[128]{0:T(128)S(1)}, u32[128]{0:T(128)}, u32[]{:S(2)}) copy-start(u32[128]{0:T(128)} %constant.244) | copy-start | bytes 1540
  293.7 116.4 %copy-start.19 = (u32[128]{0:T(128)S(1)}, u32[128]{0:T(128)}, u32[]{:S(2)}) copy-start(u32[128]{0:T(128)} %constant.240) | copy-start | bytes 1540
  293.7 117.0 %copy-start.18 = (u32[128]{0:T(128)S(1)}, u32[128]{0:T(128)}, u32[]{:S(2)}) copy-start(u32[128]{0:T(128)} %constant.236) | copy-start | bytes 1540
  293.7 117.6 %copy-start.17 = (u32[128]{0:T(128)S(1)}, u32[128]{0:T(128)}, u32[]{:S(2)}) copy-start(u32[128]{0:T(128)} %constant.232) | copy-start | bytes 1540
  293.7 70.2 %reduce-scatter.13.cloned.1.call-start = ((), (), s32[]{:S(2)}) async-start(), calls=%async_computation.18 | async-start | bytes 2621440 | tf_op jit(solution)/shard_map/reduce_scatter | solution.py:55
  294.4 92.3 %reduce-scatter.33.cloned.1.call-start = ((), (), s32[]{:S(2)}) async-start(), calls=%async_computation.28 | async-start | bytes 163840 | tf_op jit(solution)/shard_map/reduce_scatter | solution.py:55
  308.2 101.2 %reduce-scatter.27.cloned.1.call-start = ((), (), s32[]{:S(2)}) async-start(), calls=%async_computation.25 | async-start | bytes 163840 | tf_op jit(solution)/shard_map/reduce_scatter | solution.py:55
  331.8 90.0 %reduce-scatter.15.cloned.1.call-start = ((), (), s32[]{:S(2)}) async-start(), calls=%async_computation.19 | async-start | bytes 786432 | tf_op jit(solution)/shard_map/reduce_scatter | solution.py:55
  363.9 72.2 %reduce-scatter.19.cloned.1.call-start = ((), (), s32[]{:S(2)}) async-start(), calls=%async_computation.21 | async-start | bytes 786432 | tf_op jit(solution)/shard_map/reduce_scatter | solution.py:55
  365.9 83.8 %reduce-scatter.35.cloned.1.call-start = ((), (), s32[]{:S(2)}) async-start(), calls=%async_computation.29 | async-start | bytes 49152 | tf_op jit(solution)/shard_map/reduce_scatter | solution.py:55
  386.8 87.6 %reduce-scatter.29.cloned.1.call-start = ((), (), s32[]{:S(2)}) async-start(), calls=%async_computation.26 | async-start | bytes 40960 | tf_op jit(solution)/shard_map/reduce_scatter | solution.py:55
  409.4 87.3 %reduce-scatter.17.cloned.1.call-start = ((), (), s32[]{:S(2)}) async-start(), calls=%async_computation.20 | async-start | bytes 81920 | tf_op jit(solution)/shard_map/reduce_scatter | solution.py:55
  423.5 137.7 %copy-start.1 = (bf16[12,8,64,256]{3,2,1,0:T(8,128)(2,1)S(1)}, bf16[12,8,64,256]{3,2,1,0:T(8,128)(2,1)}, u32[]{:S(2)}) copy-start(bf16[12,8,64,256]{3,2,1,0:T(8,128)(2,1)} %param.19) | copy-start | bytes 9437188
  423.5 96.0 %reduce-scatter.21.cloned.1.call-start = ((), (), s32[]{:S(2)}) async-start(), calls=%async_computation.22 | async-start | bytes 327680 | tf_op jit(solution)/shard_map/reduce_scatter | solution.py:55
  436.1 106.0 %reduce-scatter.23.cloned.1.call-start = ((), (), s32[]{:S(2)}) async-start(), calls=%async_computation.23 | async-start | bytes 81920 | tf_op jit(solution)/shard_map/reduce_scatter | solution.py:55
  (15 other events, 247.8 us)
Sparse Core Ops, SparseCore 0:
  91.8 27.9 all-gather.4
  122.8 11.3 all-gather.6
  139.2 30.1 all-gather.8
  172.5 31.3 all-gather.10
  290.6 17.4 reduce-scatter.30
  310.4 21.3 reduce-scatter.24
  334.2 29.6 reduce-scatter.12
  366.2 20.4 reduce-scatter.32
  389.1 20.1 reduce-scatter.26
  411.5 10.1 reduce-scatter.14
  424.1 11.8 reduce-scatter.18
  438.2 11.5 reduce-scatter.34
  452.1 22.2 reduce-scatter.28
  476.5 20.0 reduce-scatter.16
  498.9 20.5 reduce-scatter.20
  521.7 20.3 reduce-scatter.22
